TPU v7x, 32 devices: a whole 2x2x4 slice. The times are simulated.
32 devices in a mesh: dp: 8 (over z, y), group: 4 (over x, core).
Axes of the slice: x: 2, y: 2, z: 4, core: 2. Of those that a mesh axis runs over, the one named last changes fastest.
Arguments:
- rewards: bfloat16 [8192, 4096], P(('dp', 'group')), may hold values from -6 to 6
- values: bfloat16 [8192, 4096], P(('dp', 'group')), may hold values from -6 to 6
- lengths: int32 [8192], P(('dp', 'group')), may hold values from 1 to 4096
- decay_rate: float32 [8192], P(('dp', 'group')), may hold values from 3.8146973e-06 to 0.03125
- piece_dest: int32 [8, 8], P('dp'), may hold values from 0 to 7, each once within a row
- row_perm: int32 [64, 128], P(('dp', 'group')), may hold values from 0 to 127, each once within a row
- minibatch: int32 [8192], P(('dp', 'group')), may hold values from 0 to 63
Outputs:
- white_rewards: bfloat16 [8192, 4096], P(('dp', 'group'))
- white_advantage: bfloat16 [8192, 4096], P(('dp', 'group'))
Inputs may be any that keep to these rules, and one draw needn't show every extreme that they name: Each row of piece_dest names every index of dp once. Each row of row_perm names every number below 128 once.
All inputs are finite; a program needn't handle non-finite values.
Results may differ from a plain program's by a relative error of at most 0.0049.
Values may be sent and summed in bfloat16 or wider, within the bound.
A program may use at most 64 MiB of HBM per device.

v0:
```python
import jax
import jax.numpy as jnp
from jax import lax
from jax.sharding import PartitionSpec as P

MINIBATCHES = 64
HIGHEST = lax.Precision.HIGHEST


def discounted(rewards, values, lengths, decay_rate):
    rows_here, span = rewards.shape
    block = min(128, span)
    blocks_here = span // block
    position = jnp.arange(span, dtype=jnp.int32)
    is_valid = position[None, :] < lengths[:, None]
    next_valid = position[None, :] + 1 < lengths[:, None]
    per_step = jnp.exp(-decay_rate)
    value_f = values.astype(jnp.float32)
    value_next = jnp.concatenate([value_f[:, 1:], jnp.zeros((rows_here, 1), jnp.float32)], axis=1)
    td_error = (
        rewards.astype(jnp.float32)
        + per_step[:, None] * jnp.where(next_valid, value_next, 0.0)
        - value_f
    )
    td_error = jnp.where(is_valid, td_error, 0.0).reshape(rows_here, blocks_here, block)
    offset = jnp.arange(block, dtype=jnp.float32)
    lower_scale = jnp.exp(-decay_rate[:, None] * offset[None, :])
    upper_scale = jnp.exp(decay_rate[:, None] * offset[None, :])
    triangle = (offset[:, None] >= offset[None, :]).astype(jnp.float32)
    scaled = td_error * lower_scale[:, None, :]
    summed = jnp.einsum("rjk,kt->rjt", scaled, triangle, precision=HIGHEST)
    local_part = summed * upper_scale[:, None, :]
    heads = local_part[:, :, 0]
    block_step = jnp.exp(-decay_rate * block)

    def carry_step(carry, head):
        fresh = head + block_step * carry
        return (fresh, fresh)

    final_carry, starts = lax.scan(carry_step, jnp.zeros_like(decay_rate), heads.T, reverse=True)
    next_heads = jnp.concatenate([starts[1:].T, jnp.zeros((rows_here, 1), jnp.float32)], axis=1)
    reach = jnp.exp(-decay_rate[:, None] * (block - offset[None, :]))
    total = local_part + reach[:, None, :] * next_heads[:, :, None]
    return jnp.where(is_valid, total.reshape(rows_here, span), 0.0).astype(jnp.bfloat16)


def by_target(array, piece_dest):
    peers = piece_dest.shape[1]
    target = piece_dest[0]
    slots = jnp.arange(peers, dtype=jnp.int32)
    source_slot = jnp.sum(jnp.where(target[None, :] == slots[:, None], slots[None, :], 0), axis=1)
    pieces = array.reshape((peers, array.shape[0] // peers) + array.shape[1:])
    return jnp.take(pieces, source_slot, axis=0).reshape(array.shape)


def reorder(received, row_perm):
    blocks_here, block = row_perm.shape
    chooser = (row_perm[:, :, None] == jnp.arange(block, dtype=jnp.int32)[None, None, :]).astype(
        jnp.bfloat16
    )

    def permute_one(member):
        shaped = member.reshape(blocks_here, block, member.shape[-1])
        mixed = jnp.einsum("bim,bmc->bic", chooser, shaped, preferred_element_type=jnp.float32)
        return mixed.astype(jnp.bfloat16).reshape(member.shape)

    return tuple((permute_one(member) for member in received))


def whiten(rewards, advantage, lengths, minibatch):
    rows_here, span = rewards.shape
    position = jnp.arange(span, dtype=jnp.int32)
    is_valid = position[None, :] < lengths[:, None]
    counted = lengths.astype(jnp.float32)
    reward_f = jnp.where(is_valid, rewards.astype(jnp.float32), 0.0)
    advantage_f = jnp.where(is_valid, advantage.astype(jnp.float32), 0.0)
    member = (minibatch[:, None] == jnp.arange(MINIBATCHES, dtype=jnp.int32)[None, :]).astype(
        jnp.float32
    )
    row_terms = jnp.stack(
        [
            counted,
            jnp.sum(reward_f, axis=1),
            jnp.sum(advantage_f, axis=1),
            jnp.sum(reward_f * reward_f, axis=1),
            jnp.sum(advantage_f * advantage_f, axis=1),
        ],
        axis=1,
    )
    totals = lax.psum(jnp.dot(member.T, row_terms, precision=HIGHEST), ("dp", "group"))
    count = jnp.maximum(totals[:, 0], 1.0)
    means = totals[:, 1:3] / count[:, None]
    spreads = totals[:, 3:5] / count[:, None] - means * means
    row_means = jnp.dot(member, means, precision=HIGHEST)
    row_scale = jnp.dot(member, lax.rsqrt(spreads + 1e-05), precision=HIGHEST)
    white_rewards = jnp.where(is_valid, (reward_f - row_means[:, 0:1]) * row_scale[:, 0:1], 0.0)
    white_advantage = jnp.where(
        is_valid, (advantage_f - row_means[:, 1:2]) * row_scale[:, 1:2], 0.0
    )
    return (white_rewards.astype(jnp.bfloat16), white_advantage.astype(jnp.bfloat16))


def local(rewards, values, lengths, decay_rate, piece_dest, row_perm, minibatch):
    blocks_here, block = row_perm.shape
    new_order = (jnp.arange(blocks_here, dtype=jnp.int32)[:, None] * block + row_perm).reshape(-1)
    per_row = jnp.stack([lengths.astype(jnp.float32), decay_rate], axis=1)
    moved_terms = lax.all_to_all(
        by_target(per_row, piece_dest), "dp", split_axis=0, concat_axis=0, tiled=True
    )
    moved_terms = jnp.take(moved_terms, new_order, axis=0)
    lengths_here = moved_terms[:, 0].astype(jnp.int32)
    rate_here = moved_terms[:, 1]
    moved_rewards, moved_second = reorder(
        (
            lax.all_to_all(
                by_target(rewards, piece_dest), "dp", split_axis=0, concat_axis=0, tiled=True
            ),
            lax.all_to_all(
                by_target(values, piece_dest), "dp", split_axis=0, concat_axis=0, tiled=True
            ),
        ),
        row_perm,
    )
    advantage = discounted(moved_rewards, moved_second, lengths_here, rate_here)
    return whiten(moved_rewards, advantage, lengths_here, minibatch)


def solution(mesh):
    return jax.shard_map(
        local,
        mesh=mesh,
        in_specs=(
            P(("dp", "group"), None),
            P(("dp", "group"), None),
            P(("dp", "group")),
            P(("dp", "group")),
            P("dp", None),
            P(("dp", "group"), None),
            P(("dp", "group")),
        ),
        out_specs=(P(("dp", "group"), None), P(("dp", "group"), None)),
        check_vma=False,
    )
```

profile of v0, /device:TPU:10, one launch (start us, length us, event | category | flops | bytes accessed | tf_op | source)
XLA Modules:
  0.0 195.4 jit_solution(8454684337441469848)
XLA Ops:
  0.6 0.0 copy-start
  0.6 0.9 select_reduce_fusion
  1.6 0.7 convert_element_type.58
  2.3 0.1 stack.25
  2.4 0.8 stack.26
  3.1 0.6 gather_fusion
  3.7 0.7 broadcast_select_fusion.3
  4.4 6.3 %all-to-all-start = ((f32[8,32,2]{1,2,0:T(2,128)}), f32[8,32,2]{1,2,0:T(2,128)S(1)}, u32[]{:S(2)}, u32[]{:S(2)}) async-start(f32[8,32,2]{1,2,0:T(2,128)} %broadcast_select_fusion.3), calls=%async_computation | async-start | bytes 16384 | tf_op jit(solution)/shard_map/all_to_all | solution.py:107
  10.7 0.0 copy-done
  10.7 2.0 %gather_fusion.2 = bf16[8,32,4096]{2,1,0:T(8,128)(2,1)} fusion(bf16[8,32,4096]{2,1,0:T(8,128)(2,1)S(1)} %bitcast.76, s32[1024]{0:T(1024)S(1)} %pad_clamp_fusion), kind=kCustom, calls=%fused_computation.clone | custom fusion | bytes 4194336 | tf_op jit(solution)/shard_map/jit(_take)/gather | solution.py:53
  12.7 3.6 %gather_fusion.3 = bf16[8,32,4096]{2,1,0:T(8,128)(2,1)} fusion(bf16[8,32,4096]{2,1,0:T(8,128)(2,1)} %bitcast.80, s32[1024]{0:T(1024)S(1)} %pad_clamp_fusion), kind=kCustom, calls=%fused_computation.1.clone | custom fusion | bytes 4194336 | tf_op jit(solution)/shard_map/jit(_take)/gather | solution.py:53
  16.3 4.7 %broadcast_select_fusion = (bf16[8,32,4096]{2,1,0:T(8,128)(2,1)}, bf16[8,32,4096]{2,1,0:T(8,128)(2,1)}) fusion(bf16[8,32,4096]{2,1,0:T(8,128)(2,1)} %gather_fusion.3, pred[8]{0:T(512)(128)(4,1)S(1)} %compare_and_fusion, bf16[8,32,4096]{2,1,0:T(8,128)(2,1)} %gather_fusion.2), kind=kLoop, calls=%fused_computation.37 | loop fusion | flops 2097152 | bytes 8388616 | tf_op jit(solution)/shard_map/jit(_take)/select_n | solution.py:53
  20.9 0.0 all-to-all-done
  20.9 53.1 %all_to_all.21 = bf16[8,32,4096]{2,1,0:T(8,128)(2,1)} all-to-all(bf16[8,32,4096]{2,1,0:T(8,128)(2,1)} %get-tuple-element.154), channel_id=1, replica_groups=mesh['dp'=8,'group'=4] {'dp'}, dimensions={0} | all-to-all | bytes 4194304 | tf_op jit(solution)/shard_map/all_to_all | solution.py:118
  74.0 5.2 %all-to-all-start.1 = ((bf16[8,32,4096]{2,1,0:T(8,128)(2,1)}), bf16[8,32,4096]{2,1,0:T(8,128)(2,1)}, u32[]{:S(2)}, u32[]{:S(2)}) async-start(bf16[8,32,4096]{2,1,0:T(8,128)(2,1)} %get-tuple-element.155), calls=%async_computation.1 | async-start | bytes 4194304 | tf_op jit(solution)/shard_map/all_to_all | solution.py:115
  79.2 0.0 copy-done.6
  79.2 0.1 compare_and_fusion.1
  79.3 0.1 copy.56
  79.4 0.7 gather_fusion.1
  80.2 0.1 broadcast_select_fusion.2
  80.3 0.3 fusion.21
  80.5 0.1 multiply_exponential_fusion
  80.6 0.1 copy.52
  80.7 0.1 copy.54
  80.8 0.1 fusion.20
  81.0 2.3 %convolution_convert_fusion = bf16[2,128,4096]{2,1,0:T(8,128)(2,1)S(1)} fusion(bf16[2,128,4096]{2,1,0:T(8,128)(2,1)} %bitcast.78, s32[2,128]{1,0:T(2,128)S(1)} %copy-done.6), kind=kOutput, calls=%fused_computation.9 | convolution fusion | flops 269516800 | bytes 4195328 | tf_op jit(solution)/shard_map/bim,bmc->bic/dot_general | solution.py:64
  83.3 0.0 copy-start.1
  83.3 1.3 copy-done.1
  84.6 0.6 bitcast_convert_fusion
  85.3 3.1 %slice.58 = f32[256,4095]{1,0:T(8,128)} slice(f32[256,4096]{1,0:T(8,128)S(1)} %bitcast_convert_fusion), slice={[0:256], [1:4096]} | slice | bytes 8386560 | tf_op jit(solution)/shard_map/slice | solution.py:19
  88.4 34.9 %all-to-all-done.1 = bf16[8,32,4096]{2,1,0:T(8,128)(2,1)} async-done(((bf16[8,32,4096]{2,1,0:T(8,128)(2,1)}), bf16[8,32,4096]{2,1,0:T(8,128)(2,1)}, u32[]{:S(2)}, u32[]{:S(2)}) %all-to-all-start.1) | async-done | bytes 2097184 | tf_op jit(solution)/shard_map/all_to_all | solution.py:115
  123.3 3.0 %multiply_reduce_fusion.1 = (f32[2,128]{1,0:T(2,128)S(1)}, f32[2,128]{1,0:T(2,128)S(1)}, f32[2,128,4096]{2,1,0:T(8,128)S(1)}) fusion(s32[2,128]{1,0:T(2,128)S(1)} %bitcast.84, bf16[2,128,4096]{2,1,0:T(8,128)(2,1)} %bitcast.10, s32[2,128]{1,0:T(2,128)S(1)} %copy-done.6), kind=kOutput, calls=%fused_computation.27 | convolution fusion | flops 275807744 | bytes 6295552 | tf_op jit(solution)/shard_map/bim,bmc->bic/dot_general | solution.py:64
  126.3 0.0 copy-start.4
  126.3 0.0 copy-done.2
  126.4 0.4 copy-done.5
  126.8 1.8 fusion.10
  128.6 0.0 copy-done.4
  128.6 2.9 %fusion.14 = f32[256,32,128]{0,2,1:T(8,128)S(1)} fusion(f32[256,128]{0,1:T(8,128)S(1)} %get-tuple-element.157, f32[256,128]{1,0:T(8,128)S(1)} %copy.52, f32[256,4096]{1,0:T(8,128)S(1)} %fusion.10), kind=kOutput, calls=%fused_computation.34 | convolution fusion | flops 1612726272 | bytes 8650752 | tf_op jit(solution)/shard_map/rjk,kt->rjt/dot_general | solution.py:31
  131.5 2.0 %copy-done.3 = f32[256,32,128]{0,2,1:T(8,128)} copy-done((f32[256,32,128]{0,2,1:T(8,128)}, f32[256,32,128]{0,2,1:T(8,128)S(1)}, u32[]{:S(2)}) %copy-start.3) | copy-done | bytes 4194328
  133.5 3.3 %while.17 = (s32[]{:T(128)}, f32[256]{0:T(256)S(1)}, f32[32,256]{1,0:T(8,128)S(1)}, f32[32,256]{1,0:T(8,128)S(1)}, f32[256]{0:T(256)S(1)}, /*index=5*/s32[]{:T(128)}, s32[]{:T(128)}, s32[]{:T(128)}) while((s32[]{:T(128)}, f32[256]{0:T(256)S(1)}, f32[32,256]{1,0:T(8,128)S(1)}, f32[32,256]{1,0:T(8,128)S(1)}, f32[256]{0:T(256)S(1)}, ...), condition=%wide.region_3.5_spmd.clone, body=%wide.region_2.4_spmd.clone.sunk | while | flops 772 | bytes 8307 | solution.py:40
  136.8 5.0 %multiply_reduce_fusion = (f32[256]{0:T(256)S(1)}, f32[256]{0:T(256)S(1)}, bf16[256,32,128]{0,2,1:T(8,128)(2,1)}) fusion(s32[256]{0:T(256)S(1)} %fusion.20, s32[32,128]{1,0:T(8,128)S(1)} %multiply_add_fusion.1, f32[256,32,128]{0,2,1:T(8,128)} %copy-done.3, f32[256,32]{0,1:T(8,128)S(1)} %concatenate.8, f32[256,128]{0,1:T(8,128)S(1)} %get-tuple-element.152), kind=kLoop, calls=%fused_computation.26 | loop fusion | flops 10485248 | bytes 6474752 | tf_op jit(solution)/shard_map/reduce_sum | solution.py:86
  141.9 0.2 fusion.18
  142.1 42.8 %psum.7 = f32[64,5]{0,1:T(8,128)S(1)} all-reduce(f32[64,5]{0,1:T(8,128)S(1)} %fusion.18), channel_id=1, replica_groups=mesh['dp'=8,'group'=4] {'dp','group'}, use_global_device_ids=true, to_apply=%region_7.9 | all-reduce | flops 320 | bytes 2560 | tf_op jit(solution)/shard_map/psum | solution.py:90
  184.9 0.2 fusion.17
  185.1 0.3 fusion.16
  185.3 0.1 fusion.37
  185.4 4.1 %copy.55 = bf16[256,4096]{1,0:T(8,128)(2,1)} copy(bf16[256,4096]{0,1:T(8,128)(2,1)} %bitcast.79) | data formatting | bytes 4194304 | tf_op jit(solution)/shard_map/reshape | solution.py:44
  189.5 5.9 %select_convert_fusion = (bf16[256,4096]{1,0:T(8,128)(2,1)}, bf16[256,4096]{1,0:T(8,128)(2,1)}) fusion(bf16[256,4096]{1,0:T(8,128)(2,1)} %copy.55, f32[256]{0:T(256)S(1)} %bitcast.89, f32[256]{0:T(256)S(1)} %bitcast.87, s32[256]{0:T(256)S(1)} %fusion.20, f32[256]{0:T(256)S(1)} %bitcast.90, f32[256]{0:T(256)S(1)} %bitcast.88, f32[2,128,4096]{2,1,0:T(8,128)} %copy-done.4), kind=kLoop, calls=%fused_computation.24 | loop fusion | flops 13631488 | bytes 10490880 | tf_op jit(solution)/shard_map/convert_element_type | solution.py:100
  (124 shorter events, 2.3 us)
Async XLA Ops:
  0.6 10.0 %copy-start = (bf16[256,4096]{1,0:T(8,128)(2,1)S(1)}, bf16[256,4096]{1,0:T(8,128)(2,1)}, u32[]{:S(2)}) copy-start(bf16[256,4096]{1,0:T(8,128)(2,1)} %param.11) | copy-start | bytes 6291460
  4.4 16.6 %all-to-all-start = ((f32[8,32,2]{1,2,0:T(2,128)}), f32[8,32,2]{1,2,0:T(2,128)S(1)}, u32[]{:S(2)}, u32[]{:S(2)}) async-start(f32[8,32,2]{1,2,0:T(2,128)} %broadcast_select_fusion.3), calls=%async_computation | async-start | bytes 16384 | tf_op jit(solution)/shard_map/all_to_all | solution.py:107
  20.9 58.2 %copy-start.6 = (s32[2,128]{1,0:T(2,128)S(1)}, s32[2,128]{1,0:T(2,128)}, u32[]{:S(2)}) copy-start(s32[2,128]{1,0:T(2,128)} %param.16) | copy-start | bytes 3076
  74.0 49.3 %all-to-all-start.1 = ((bf16[8,32,4096]{2,1,0:T(8,128)(2,1)}), bf16[8,32,4096]{2,1,0:T(8,128)(2,1)}, u32[]{:S(2)}, u32[]{:S(2)}) async-start(bf16[8,32,4096]{2,1,0:T(8,128)(2,1)} %get-tuple-element.155), calls=%async_computation.1 | async-start | bytes 4194304 | tf_op jit(solution)/shard_map/all_to_all | solution.py:115
  83.3 1.3 copy-start.1
  123.3 3.0 %copy-start.2 = (bf16[2,128,4096]{2,1,0:T(8,128)(2,1)S(1)}, bf16[2,128,4096]{2,1,0:T(8,128)(2,1)}, u32[]{:S(2)}) copy-start(bf16[2,128,4096]{2,1,0:T(8,128)(2,1)} %copy-done.1) | copy-start | bytes 6291460
  123.3 3.5 %copy-start.5 = (f32[256,4095]{1,0:T(8,128)S(1)}, f32[256,4095]{1,0:T(8,128)}, u32[]{:S(2)}) copy-start(f32[256,4095]{1,0:T(8,128)} %slice.58) | copy-start | bytes 12579844
  126.3 2.2 %copy-start.4 = (f32[2,128,4096]{2,1,0:T(8,128)}, f32[2,128,4096]{2,1,0:T(8,128)S(1)}, u32[]{:S(2)}) copy-start(f32[2,128,4096]{2,1,0:T(8,128)S(1)} %get-tuple-element.156) | copy-start | bytes 12582916
  131.5 2.0 %copy-start.3 = (f32[256,32,128]{0,2,1:T(8,128)}, f32[256,32,128]{0,2,1:T(8,128)S(1)}, u32[]{:S(2)}) copy-start(f32[256,32,128]{0,2,1:T(8,128)S(1)} %fusion.14) | copy-start | bytes 12582916
  133.4 8.4 %copy-start.7 = (s32[256]{0:T(256)S(1)}, s32[256]{0:T(256)}, u32[]{:S(2)}) copy-start(s32[256]{0:T(256)} %param.17) | copy-start | bytes 3076
where the time goes:
time: 196 us; the launch traced here: 195 us
  blocking collectives  95.8 us (49%)
  waiting for transfers between devices  34.9 us (18%)
  other arithmetic  21.5 us (11%)
  local copies, waits for them, and re-layouts  20.8 us (11%)
  starting transfers between devices  11.4 us (6%)
  matrix products  8.91 us (5%)
    all_to_all x1, blocking collectives, local(): lax.all_to_all(by_target(values, piece_dest), 'dp', split_axis=0, concat_...  53.1 us
    psum x1, blocking collectives, whiten(): lax.psum(jnp.dot(member.T, row_terms, precision=HIGHEST), ('dp', 'group'))  42.8 us
    all_to_all x1, waiting for transfers between devices, local(): lax.all_to_all(by_target(rewards, piece_dest), 'dp', split_axis=0, concat...  34.9 us
    all_to_all x1, starting transfers between devices, local(): lax.all_to_all(by_target(per_row, piece_dest), 'dp', split_axis=0, concat...  6.28 us
    gather x3, local copies, waits for them, and re-layouts, by_target(): return jnp.take(pieces, source_slot, axis=0).reshape(array.shape)  6.16 us
    convert_element_type x1, other arithmetic, whiten(): white_advantage.astype(jnp.bfloat16)  5.93 us
    dot_general x2, matrix products, permute_one(): jnp.einsum('bim,bmc->bic', chooser, shaped, preferred_element_type=jnp.fl...  5.36 us
    select_n x4, other arithmetic, by_target(): return jnp.take(pieces, source_slot, axis=0).reshape(array.shape)  5.35 us
  transfers between devices with their start and end apart: 2, of which 1 were waited for; matrix products, arithmetic and copies ran while one was open for 9% of the time, Pallas kernels for 0%

commit v1 on v0

--- a/solution.py
+++ b/solution.py
@@ -87,7 +87,8 @@
         ],
         axis=1,
     )
-    totals = lax.psum(jnp.dot(member.T, row_terms, precision=HIGHEST), ("dp", "group"))
+    inner = lax.psum(jnp.dot(member.T, row_terms, precision=HIGHEST), "group")
+    totals = lax.psum(inner, "dp")
     count = jnp.maximum(totals[:, 0], 1.0)
     means = totals[:, 1:3] / count[:, None]
     spreads = totals[:, 3:5] / count[:, None] - means * means

time: 196 us -> 184 us (0.939)
  the two profiles are of different devices: /device:TPU:10 before, /device:TPU:0 now
where the time goes in v1:
time: 184 us; the launch traced here: 183 us
  blocking collectives  80.3 us (44%)
  waiting for transfers between devices  38 us (21%)
  other arithmetic  21.5 us (12%)
  local copies, waits for them, and re-layouts  20.8 us (11%)
  starting transfers between devices  11.7 us (6%)
  matrix products  8.91 us (5%)
    all_to_all x1, blocking collectives, local(): lax.all_to_all(by_target(values, piece_dest), 'dp', split_axis=0, concat_...  54 us
    all_to_all x1, waiting for transfers between devices, local(): lax.all_to_all(by_target(rewards, piece_dest), 'dp', split_axis=0, concat...  38 us
    psum x1, blocking collectives, whiten(): totals = lax.psum(inner, 'dp')  20.7 us
    all_to_all x1, starting transfers between devices, local(): lax.all_to_all(by_target(per_row, piece_dest), 'dp', split_axis=0, concat...  7.31 us
    gather x3, local copies, waits for them, and re-layouts, by_target(): return jnp.take(pieces, source_slot, axis=0).reshape(array.shape)  6.16 us
    convert_element_type x1, other arithmetic, whiten(): white_advantage.astype(jnp.bfloat16)  5.93 us
    psum x1, blocking collectives, whiten(): inner = lax.psum(jnp.dot(member.T, row_terms, precision=HIGHEST), 'group')  5.65 us
    dot_general x2, matrix products, permute_one(): jnp.einsum('bim,bmc->bic', chooser, shaped, preferred_element_type=jnp.fl...  5.35 us
  transfers between devices with their start and end apart: 2, of which 1 were waited for; matrix products, arithmetic and copies ran while one was open for 10% of the time, Pallas kernels for 0%

profile of v1, /device:TPU:0, one launch (start us, length us, event | category | flops | bytes accessed | tf_op | source)
XLA Modules:
  0.0 183.2 jit_solution(14429782176399896438)
XLA Ops:
  0.6 0.0 copy-start
  0.6 0.9 select_reduce_fusion
  1.6 0.7 convert_element_type.58
  2.3 0.1 stack.25
  2.4 0.8 stack.26
  3.1 0.6 gather_fusion
  3.7 0.7 broadcast_select_fusion.3
  4.4 7.3 %all-to-all-start = ((f32[8,32,2]{1,2,0:T(2,128)}), f32[8,32,2]{1,2,0:T(2,128)S(1)}, u32[]{:S(2)}, u32[]{:S(2)}) async-start(f32[8,32,2]{1,2,0:T(2,128)} %broadcast_select_fusion.3), calls=%async_computation | async-start | bytes 16384 | tf_op jit(solution)/shard_map/all_to_all | solution.py:108
  11.7 0.0 copy-done
  11.7 2.0 %gather_fusion.2 = bf16[8,32,4096]{2,1,0:T(8,128)(2,1)} fusion(bf16[8,32,4096]{2,1,0:T(8,128)(2,1)S(1)} %bitcast.76, s32[1024]{0:T(1024)S(1)} %pad_clamp_fusion), kind=kCustom, calls=%fused_computation.clone | custom fusion | bytes 4194336 | tf_op jit(solution)/shard_map/jit(_take)/gather | solution.py:53
  13.7 3.6 %gather_fusion.3 = bf16[8,32,4096]{2,1,0:T(8,128)(2,1)} fusion(bf16[8,32,4096]{2,1,0:T(8,128)(2,1)} %bitcast.80, s32[1024]{0:T(1024)S(1)} %pad_clamp_fusion), kind=kCustom, calls=%fused_computation.1.clone | custom fusion | bytes 4194336 | tf_op jit(solution)/shard_map/jit(_take)/gather | solution.py:53
  17.3 4.7 %broadcast_select_fusion = (bf16[8,32,4096]{2,1,0:T(8,128)(2,1)}, bf16[8,32,4096]{2,1,0:T(8,128)(2,1)}) fusion(bf16[8,32,4096]{2,1,0:T(8,128)(2,1)} %gather_fusion.3, pred[8]{0:T(512)(128)(4,1)S(1)} %compare_and_fusion, bf16[8,32,4096]{2,1,0:T(8,128)(2,1)} %gather_fusion.2), kind=kLoop, calls=%fused_computation.37 | loop fusion | flops 2097152 | bytes 8388616 | tf_op jit(solution)/shard_map/jit(_take)/select_n | solution.py:53
  22.0 0.0 all-to-all-done
  22.0 54.0 %all_to_all.21 = bf16[8,32,4096]{2,1,0:T(8,128)(2,1)} all-to-all(bf16[8,32,4096]{2,1,0:T(8,128)(2,1)} %get-tuple-element.154), channel_id=1, replica_groups=mesh['dp'=8,'group'=4] {'dp'}, dimensions={0} | all-to-all | bytes 4194304 | tf_op jit(solution)/shard_map/all_to_all | solution.py:119
  76.0 4.3 %all-to-all-start.1 = ((bf16[8,32,4096]{2,1,0:T(8,128)(2,1)}), bf16[8,32,4096]{2,1,0:T(8,128)(2,1)}, u32[]{:S(2)}, u32[]{:S(2)}) async-start(bf16[8,32,4096]{2,1,0:T(8,128)(2,1)} %get-tuple-element.155), calls=%async_computation.1 | async-start | bytes 4194304 | tf_op jit(solution)/shard_map/all_to_all | solution.py:116
  80.4 0.0 copy-done.6
  80.4 0.1 compare_and_fusion.1
  80.5 0.1 copy.56
  80.6 0.7 gather_fusion.1
  81.3 0.1 broadcast_select_fusion.2
  81.4 0.3 fusion.21
  81.7 0.1 multiply_exponential_fusion
  81.8 0.1 copy.52
  81.9 0.1 copy.54
  82.0 0.1 fusion.20
  82.1 2.3 %convolution_convert_fusion = bf16[2,128,4096]{2,1,0:T(8,128)(2,1)S(1)} fusion(bf16[2,128,4096]{2,1,0:T(8,128)(2,1)} %bitcast.78, s32[2,128]{1,0:T(2,128)S(1)} %copy-done.6), kind=kOutput, calls=%fused_computation.9 | convolution fusion | flops 269516800 | bytes 4195328 | tf_op jit(solution)/shard_map/bim,bmc->bic/dot_general | solution.py:64
  84.5 0.0 copy-start.1
  84.5 1.3 copy-done.1
  85.8 0.6 bitcast_convert_fusion
  86.4 3.1 %slice.58 = f32[256,4095]{1,0:T(8,128)} slice(f32[256,4096]{1,0:T(8,128)S(1)} %bitcast_convert_fusion), slice={[0:256], [1:4096]} | slice | bytes 8386560 | tf_op jit(solution)/shard_map/slice | solution.py:19
  89.5 38.0 %all-to-all-done.1 = bf16[8,32,4096]{2,1,0:T(8,128)(2,1)} async-done(((bf16[8,32,4096]{2,1,0:T(8,128)(2,1)}), bf16[8,32,4096]{2,1,0:T(8,128)(2,1)}, u32[]{:S(2)}, u32[]{:S(2)}) %all-to-all-start.1) | async-done | bytes 2097184 | tf_op jit(solution)/shard_map/all_to_all | solution.py:116
  127.6 3.0 %multiply_reduce_fusion.1 = (f32[2,128]{1,0:T(2,128)S(1)}, f32[2,128]{1,0:T(2,128)S(1)}, f32[2,128,4096]{2,1,0:T(8,128)S(1)}) fusion(s32[2,128]{1,0:T(2,128)S(1)} %bitcast.84, bf16[2,128,4096]{2,1,0:T(8,128)(2,1)} %bitcast.10, s32[2,128]{1,0:T(2,128)S(1)} %copy-done.6), kind=kOutput, calls=%fused_computation.27 | convolution fusion | flops 275807744 | bytes 6295552 | tf_op jit(solution)/shard_map/bim,bmc->bic/dot_general | solution.py:64
  130.6 0.0 copy-start.4
  130.6 0.0 copy-done.2
  130.6 0.4 copy-done.5
  131.0 1.8 fusion.10
  132.8 2.9 %fusion.14 = f32[256,32,128]{0,2,1:T(8,128)S(1)} fusion(f32[256,128]{0,1:T(8,128)S(1)} %get-tuple-element.157, f32[256,128]{1,0:T(8,128)S(1)} %copy.52, f32[256,4096]{1,0:T(8,128)S(1)} %fusion.10), kind=kOutput, calls=%fused_computation.34 | convolution fusion | flops 1612726272 | bytes 8650752 | tf_op jit(solution)/shard_map/rjk,kt->rjt/dot_general | solution.py:31
  135.7 2.0 %copy-done.3 = f32[256,32,128]{0,2,1:T(8,128)} copy-done((f32[256,32,128]{0,2,1:T(8,128)}, f32[256,32,128]{0,2,1:T(8,128)S(1)}, u32[]{:S(2)}) %copy-start.3) | copy-done | bytes 4194328
  137.7 3.3 %while.17 = (s32[]{:T(128)}, f32[256]{0:T(256)S(1)}, f32[32,256]{1,0:T(8,128)S(1)}, f32[32,256]{1,0:T(8,128)S(1)}, f32[256]{0:T(256)S(1)}, /*index=5*/s32[]{:T(128)}, s32[]{:T(128)}, s32[]{:T(128)}) while((s32[]{:T(128)}, f32[256]{0:T(256)S(1)}, f32[32,256]{1,0:T(8,128)S(1)}, f32[32,256]{1,0:T(8,128)S(1)}, f32[256]{0:T(256)S(1)}, ...), condition=%wide.region_3.5_spmd.clone, body=%wide.region_2.4_spmd.clone.sunk | while | flops 772 | bytes 8307 | solution.py:40
  141.0 5.0 %multiply_reduce_fusion = (f32[256]{0:T(256)S(1)}, f32[256]{0:T(256)S(1)}, bf16[256,32,128]{0,2,1:T(8,128)(2,1)}) fusion(s32[256]{0:T(256)S(1)} %fusion.20, s32[32,128]{1,0:T(8,128)S(1)} %multiply_add_fusion.1, f32[256,32,128]{0,2,1:T(8,128)} %copy-done.3, f32[256,32]{0,1:T(8,128)S(1)} %concatenate.8, f32[256,128]{0,1:T(8,128)S(1)} %get-tuple-element.152), kind=kLoop, calls=%fused_computation.26 | loop fusion | flops 10485248 | bytes 6474752 | tf_op jit(solution)/shard_map/reduce_sum | solution.py:86
  146.1 0.2 fusion.18
  146.3 5.6 %psum.14 = f32[64,5]{0,1:T(8,128)S(1)} all-reduce(f32[64,5]{0,1:T(8,128)S(1)} %fusion.18), channel_id=1, replica_groups=mesh['dp'=8,'group'=4] {'group'}, use_global_device_ids=true, to_apply=%region_7.9 | all-reduce | flops 320 | bytes 2560 | tf_op jit(solution)/shard_map/psum | solution.py:90
  152.0 20.7 %psum.15 = f32[64,5]{0,1:T(8,128)S(1)} all-reduce(f32[64,5]{0,1:T(8,128)S(1)} %psum.14), channel_id=1, replica_groups=mesh['dp'=8,'group'=4] {'dp'}, use_global_device_ids=true, to_apply=%region_8.10 | all-reduce | flops 320 | bytes 2560 | tf_op jit(solution)/shard_map/psum | solution.py:91
  172.6 0.2 fusion.17
  172.8 0.3 fusion.16
  173.1 0.1 fusion.37
  173.2 4.1 %copy.55 = bf16[256,4096]{1,0:T(8,128)(2,1)} copy(bf16[256,4096]{0,1:T(8,128)(2,1)} %bitcast.79) | data formatting | bytes 4194304 | tf_op jit(solution)/shard_map/reshape | solution.py:44
  177.3 5.9 %select_convert_fusion = (bf16[256,4096]{1,0:T(8,128)(2,1)}, bf16[256,4096]{1,0:T(8,128)(2,1)}) fusion(bf16[256,4096]{1,0:T(8,128)(2,1)} %copy.55, f32[256]{0:T(256)S(1)} %bitcast.89, f32[256]{0:T(256)S(1)} %bitcast.87, s32[256]{0:T(256)S(1)} %fusion.20, f32[256]{0:T(256)S(1)} %bitcast.90, f32[256]{0:T(256)S(1)} %bitcast.88, f32[2,128,4096]{2,1,0:T(8,128)} %copy-done.4), kind=kLoop, calls=%fused_computation.24 | loop fusion | flops 13631488 | bytes 10490880 | tf_op jit(solution)/shard_map/convert_element_type | solution.py:101
  (125 shorter events, 2.3 us)
Async XLA Ops:
  0.6 11.1 %copy-start = (bf16[256,4096]{1,0:T(8,128)(2,1)S(1)}, bf16[256,4096]{1,0:T(8,128)(2,1)}, u32[]{:S(2)}) copy-start(bf16[256,4096]{1,0:T(8,128)(2,1)} %param.11) | copy-start | bytes 6291460
  4.4 17.6 %all-to-all-start = ((f32[8,32,2]{1,2,0:T(2,128)}), f32[8,32,2]{1,2,0:T(2,128)S(1)}, u32[]{:S(2)}, u32[]{:S(2)}) async-start(f32[8,32,2]{1,2,0:T(2,128)} %broadcast_select_fusion.3), calls=%async_computation | async-start | bytes 16384 | tf_op jit(solution)/shard_map/all_to_all | solution.py:108
  22.0 58.4 %copy-start.6 = (s32[2,128]{1,0:T(2,128)S(1)}, s32[2,128]{1,0:T(2,128)}, u32[]{:S(2)}) copy-start(s32[2,128]{1,0:T(2,128)} %param.16) | copy-start | bytes 3076
  76.0 51.6 %all-to-all-start.1 = ((bf16[8,32,4096]{2,1,0:T(8,128)(2,1)}), bf16[8,32,4096]{2,1,0:T(8,128)(2,1)}, u32[]{:S(2)}, u32[]{:S(2)}) async-start(bf16[8,32,4096]{2,1,0:T(8,128)(2,1)} %get-tuple-element.155), calls=%async_computation.1 | async-start | bytes 4194304 | tf_op jit(solution)/shard_map/all_to_all | solution.py:116
  84.5 1.3 copy-start.1
  127.6 3.0 %copy-start.2 = (bf16[2,128,4096]{2,1,0:T(8,128)(2,1)S(1)}, bf16[2,128,4096]{2,1,0:T(8,128)(2,1)}, u32[]{:S(2)}) copy-start(bf16[2,128,4096]{2,1,0:T(8,128)(2,1)} %copy-done.1) | copy-start | bytes 6291460
  127.6 3.5 %copy-start.5 = (f32[256,4095]{1,0:T(8,128)S(1)}, f32[256,4095]{1,0:T(8,128)}, u32[]{:S(2)}) copy-start(f32[256,4095]{1,0:T(8,128)} %slice.58) | copy-start | bytes 12579844
  130.6 2.3 %copy-start.4 = (f32[2,128,4096]{2,1,0:T(8,128)}, f32[2,128,4096]{2,1,0:T(8,128)S(1)}, u32[]{:S(2)}) copy-start(f32[2,128,4096]{2,1,0:T(8,128)S(1)} %get-tuple-element.156) | copy-start | bytes 12582916
  135.7 2.0 %copy-start.3 = (f32[256,32,128]{0,2,1:T(8,128)}, f32[256,32,128]{0,2,1:T(8,128)S(1)}, u32[]{:S(2)}) copy-start(f32[256,32,128]{0,2,1:T(8,128)S(1)} %fusion.14) | copy-start | bytes 12582916
  137.7 8.4 %copy-start.7 = (s32[256]{0:T(256)S(1)}, s32[256]{0:T(256)}, u32[]{:S(2)}) copy-start(s32[256]{0:T(256)} %param.17) | copy-start | bytes 3076
